TPU v7x, 512 devices: a whole 4x4x16 slice. The times are simulated.
512 devices in a mesh: row: 8 (over z_hi, core), col: 16 (over y, z_lo), dp: 4 (over x).
Axes of the slice: x: 4, y: 4, z: 16 (z_hi: 4, z_lo: 4; z = z_hi * 4 + z_lo), core: 2. Of those that a mesh axis runs over, the one named last changes fastest.
Arguments:
- activations: bfloat16 [4, 1024, 16384], P('dp', 'col', 'row'), may hold values from -6 to 6
- out_grads: bfloat16 [4, 1024, 4096], P('dp', 'row', 'col'), may hold values from -6 to 6
- block_mask: int32 [128, 32], P('row', 'col'), may hold values from 0 to 1, as said below
- master_weight: float32 [16384, 4096], P(('row', 'dp'), 'col'), may hold values from -0.046875 to 0.046875
- first_moment: float32 [16384, 4096], P(('row', 'dp'), 'col'), may hold values from -12 to 12
- second_moment: float32 [16384, 4096], P(('row', 'dp'), 'col'), may hold values from 0.05 to 2
Outputs:
- input_grads: bfloat16 [4, 1024, 16384], P('dp', 'col', 'row')
- new_weight: float32 [16384, 4096], P(('row', 'dp'), 'col')
- new_first: float32 [16384, 4096], P(('row', 'dp'), 'col')
- new_second: float32 [16384, 4096], P(('row', 'dp'), 'col')
Inputs may be any that keep to these rules, and one draw needn't show every extreme that they name: `block_mask`: 1 where the 128 x 128 block of the weight is kept, 0 where it is pruned.
All inputs are finite; a program needn't handle non-finite values.
Results may differ from a plain program's by a relative error of at most 0.015.
Values may be sent and summed in bfloat16 or wider, within the bound.
No kernel may reach another device: no remote copies, remote signals or barrier semaphores. Data moves between devices by JAX's collectives and lax.ppermute only.
A program may use at most 64 MiB of HBM per device.

v0:
```python
import jax
import jax.numpy as jnp
from jax import lax
from jax.sharding import Mesh
from jax.sharding import PartitionSpec as P

BLOCK = 128
ROW = ("row_0", "row_1")
ROW_DP = ("row_0", "row_1", "dp")
first_decay = 0.9
second_decay = 0.999
learn_rate = 0.001
adam_epsilon = 1e-08
first_correct = 1.0 - 0.9**10
second_correct = 1.0 - 0.999**10


def from_everyone(array, axis):
    copies = jnp.broadcast_to(array, (lax.axis_size(axis), *array.shape))
    return lax.all_to_all(copies, axis, split_axis=0, concat_axis=0, tiled=True)


def in_order(pieces, dim):
    dims = list(pieces.shape[1:])
    dims[dim] *= pieces.shape[0]
    return jnp.moveaxis(pieces, 0, dim).reshape(dims)


def gather_directly(array, axis, dim):
    pieces = from_everyone(array, axis)
    return in_order(pieces, dim)


def stacked_from(array, axes, sequence):
    pieces = array
    for k in sequence:
        pieces = lax.all_gather(pieces, axes[k])
    done = sequence[::-1]
    back = [done.index(k) for k in range(len(axes))]
    pieces = pieces.transpose(*back, *range(len(axes), pieces.ndim))
    return pieces.reshape(-1, *array.shape)


def gathered_by_axis(array, axes, sequence, dim):
    return in_order(stacked_from(array, axes, sequence), dim)


def split_up(array, dim, peers):
    before, after = (array.shape[:dim], array.shape[dim + 1 :])
    return jnp.moveaxis(array.reshape(*before, peers, -1, *after), dim, 0)


def summed_on_arrival(array, axis, dim):
    peers = lax.axis_size(axis)
    pieces = lax.all_to_all(split_up(array, dim, peers), axis, 0, 0, tiled=True)
    return jnp.sum(pieces.astype(jnp.float32), axis=0)


def expand(block_keep):
    tall, broad = block_keep.shape
    values = block_keep.astype(jnp.float32)
    grown = jnp.broadcast_to(values[:, None, :, None], (tall, BLOCK, broad, BLOCK))
    return grown.reshape(tall * BLOCK, broad * BLOCK)


def body(activations, out_grads, block_mask, master_weight, first_moment, second_moment):
    shard_rows = master_weight.shape[0]
    group_index = lax.axis_index("dp")
    keep_tile = expand(block_mask)
    keep_shard = lax.dynamic_slice_in_dim(keep_tile, group_index * shard_rows, shard_rows, 0)
    weight_tile = gather_directly(master_weight.astype(jnp.bfloat16), "dp", 0)
    weight_tile = weight_tile * keep_tile.astype(jnp.bfloat16)
    grad_group = gathered_by_axis(out_grads[0], ROW, (0, 1), 0)
    picked = grad_group
    tile_grad = (
        lax.dot_general(
            lax.all_gather(activations[0], "col", axis=0, tiled=True),
            picked,
            (((0,), (0,)), ((), ())),
            preferred_element_type=jnp.float32,
        )
        * keep_tile
    )
    grads_after, tile_grad = lax.optimization_barrier((grad_group, tile_grad))
    picked = grads_after
    summed_inputs = lax.psum_scatter(
        lax.dot_general(
            picked, weight_tile, (((1,), (1,)), ((), ())), preferred_element_type=jnp.float32
        ).astype(jnp.bfloat16),
        "col",
        scatter_dimension=0,
        tiled=True,
    )
    input_grads = summed_inputs[None]
    grad_shard = summed_on_arrival(tile_grad.astype(jnp.bfloat16), "dp", 0)
    new_first = first_decay * first_moment + (1.0 - first_decay) * grad_shard
    new_second = second_decay * second_moment + (1.0 - second_decay) * grad_shard * grad_shard
    step_size = new_first / first_correct / (jnp.sqrt(new_second / second_correct) + adam_epsilon)
    new_weight = keep_shard * (master_weight - learn_rate * step_size)
    return (input_grads, new_weight, new_first, new_second)


def solution(mesh):
    finer = Mesh(
        mesh.devices.reshape(4, 2, mesh.shape["col"], mesh.shape["dp"]),
        ("row_0", "row_1", "col", "dp"),
    )
    in_specs = (
        P("dp", "col", ROW),
        P("dp", ROW, "col"),
        P(ROW, "col"),
        P(ROW_DP, "col"),
        P(ROW_DP, "col"),
        P(ROW_DP, "col"),
    )
    out_specs = (P("dp", "col", ROW), P(ROW_DP, "col"), P(ROW_DP, "col"), P(ROW_DP, "col"))
    return jax.shard_map(body, mesh=finer, in_specs=in_specs, out_specs=out_specs, check_vma=False)
```

profile of v0, /device:TPU:2, one launch (start us, length us, event | category | flops | bytes accessed | tf_op | source)
XLA Modules:
  0.0 281.5 jit_solution(17840305256738993621)
XLA Ops:
  7.2 0.0 copy-start.2
  7.2 0.0 all-gather.4.cloned.1.call-start
  7.2 0.7 all-gather.4.cloned.1.call-update
  7.9 27.1 %all_gather.12 = bf16[4,128,256]{2,1,0:T(8,128)(2,1)S(1)} all-gather(bf16[1,128,256]{2,1,0:T(8,128)(2,1)} %param.7), channel_id=1, replica_groups=mesh['row_0'=4,'row_1'=2,'col'=16,'dp'=4] {'row_0'}, dimensions={0}, use_global_device_ids=true | all-gather | bytes 327680 | tf_op jit(solution)/shard_map/all_gather | solution.py:37
  35.0 2.2 all-gather
  37.2 0.0 copy-done.2
  37.3 0.0 copy-start
  37.3 0.1 copy.15
  37.4 85.1 %all-gather.4.cloned.1.call-done = bf16[1,1024,2048]{2,1,0:T(8,128)(2,1)} async-done(((bf16[1,64,2048]{2,1,0:T(8,128)(2,1)}), bf16[1,1024,2048]{2,1,0:T(8,128)(2,1)}) %all-gather.4.cloned.1.call-update) | async-done | bytes 4194320 | tf_op jit(solution)/shard_map/all_gather | solution.py:77
  122.4 0.6 broadcast_in_dim.12
  123.0 4.5 %fusion.2 = bf16[2048,256]{1,0:T(8,128)(2,1)} fusion(bf16[1024,256]{1,0:T(8,128)(2,1)S(1)} %bitcast.28, bf16[1,1024,2048]{2,1,0:T(8,128)(2,1)} %all-gather.4.cloned.1.call-done, f32[256,8,2,128]{3,2,1,0:T(2,128)S(1)} %bitcast.25), kind=kOutput, calls=%fused_computation.3 | convolution fusion | flops 1074790400 | bytes 7864320 | tf_op jit(solution)/shard_map/dot_general | solution.py:76
  127.6 0.0 copy-done
  127.6 4.8 %all-to-all-start.1 = ((bf16[4,512,256]{2,1,0:T(8,128)(2,1)}), bf16[4,512,256]{2,1,0:T(8,128)(2,1)S(1)}, u32[]{:S(2)}, u32[]{:S(2)}) async-start(bf16[4,512,256]{2,1,0:T(8,128)(2,1)} %bitcast.32), calls=%async_computation.2 | async-start | bytes 2097152 | tf_op jit(solution)/shard_map/all_to_all | solution.py:55
  132.4 0.0 reduce-scatter.2.cloned.1.call-start
  132.4 1.5 copy.22
  133.9 12.2 %all-to-all-done.1 = bf16[4,512,256]{2,1,0:T(8,128)(2,1)S(1)} async-done(((bf16[4,512,256]{2,1,0:T(8,128)(2,1)}), bf16[4,512,256]{2,1,0:T(8,128)(2,1)S(1)}, u32[]{:S(2)}, u32[]{:S(2)}) %all-to-all-start.1) | async-done | bytes 1048608 | tf_op jit(solution)/shard_map/all_to_all | solution.py:55
  146.0 0.1 convert_reduce_fusion
  146.2 3.1 %subtract_multiply_fusion = (f32[512,256]{1,0:T(8,128)}, f32[512,256]{1,0:T(8,128)}, f32[512,256]{1,0:T(8,128)}, bf16[512,256]{1,0:T(8,128)(2,1)S(1)}) fusion(f32[512,256]{1,0:T(8,128)} %param.9, f32[2048,256]{1,0:T(8,128)} %bitcast.30, s32[]{:T(128)S(6)} %select_n.3, f32[512,256]{1,0:T(8,128)S(1)} %convert_reduce_fusion, f32[512,256]{1,0:T(8,128)} %param.10, ...), kind=kLoop, calls=%fused_computation.9 | loop fusion | flops 1966080 | bytes 4456452 | tf_op jit(solution)/shard_map/mul | solution.py:99
  149.3 0.1 broadcast_in_dim.13
  149.3 16.7 %all_to_all.10 = bf16[4,512,256]{2,1,0:T(8,128)(2,1)S(1)} all-to-all(bf16[4,512,256]{2,1,0:T(8,128)(2,1)S(1)} %broadcast_in_dim.13), channel_id=1, replica_groups=mesh['row_0'=4,'row_1'=2,'col'=16,'dp'=4] {'dp'}, dimensions={0} | all-to-all | bytes 2097152 | tf_op jit(solution)/shard_map/all_to_all | solution.py:20
  166.0 0.0 copy-start.1
  166.0 0.2 bitcast_multiply_fusion
  166.2 0.8 copy-done.1
  167.1 3.2 %convolution_convert_fusion = bf16[1024,2048]{1,0:T(8,128)(2,1)} fusion(bf16[1024,256]{1,0:T(8,128)(2,1)S(1)} %bitcast.29, bf16[2048,256]{1,0:T(8,128)(2,1)S(1)} %bitcast_multiply_fusion), kind=kOutput, calls=%fused_computation.2 | convolution fusion | flops 1075838976 | bytes 5767168 | tf_op jit(solution)/shard_map/dot_general | solution.py:87
  170.3 0.0 reduce-scatter.2.cloned.1.call-update
  170.3 104.3 %reduce-scatter.2.cloned.1.call-done = bf16[64,2048]{1,0:T(8,128)(2,1)} async-done(((bf16[1024,2048]{1,0:T(8,128)(2,1)}), bf16[64,2048]{1,0:T(8,128)(2,1)}) %reduce-scatter.2.cloned.1.call-update) | async-done | bytes 262160 | tf_op jit(solution)/shard_map/reduce_scatter | solution.py:86
  (2 shorter events, 0.0 us)
Async XLA Ops:
  7.2 30.1 %copy-start.2 = (s32[16,2]{0,1:T(2,128)S(1)}, s32[16,2]{0,1:T(2,128)}, u32[]{:S(2)}) copy-start(s32[16,2]{0,1:T(2,128)} %param.8) | copy-start | bytes 388
  7.2 115.2 %all-gather.4.cloned.1.call-start = ((), (), s32[]{:S(2)}) async-start(), calls=%async_computation.4 | async-start | bytes 4456448 | tf_op jit(solution)/shard_map/all_gather | solution.py:77
  37.3 90.3 %copy-start = (bf16[4,2,128,256]{3,2,1,0:T(8,128)(2,1)}, bf16[4,2,128,256]{3,2,1,0:T(8,128)(2,1)S(1)}, u32[]{:S(2)}) copy-start(bf16[4,2,128,256]{3,2,1,0:T(8,128)(2,1)S(1)} %copy.14) | copy-start | bytes 1572868
  127.6 18.5 %all-to-all-start.1 = ((bf16[4,512,256]{2,1,0:T(8,128)(2,1)}), bf16[4,512,256]{2,1,0:T(8,128)(2,1)S(1)}, u32[]{:S(2)}, u32[]{:S(2)}) async-start(bf16[4,512,256]{2,1,0:T(8,128)(2,1)} %bitcast.32), calls=%async_computation.2 | async-start | bytes 2097152 | tf_op jit(solution)/shard_map/all_to_all | solution.py:55
  132.4 142.2 %reduce-scatter.2.cloned.1.call-start = ((), (), s32[]{:S(2)}) async-start(), calls=%async_computation.3 | async-start | bytes 4456448 | tf_op jit(solution)/shard_map/reduce_scatter | solution.py:86
  166.0 1.0 copy-start.1
Sparse Core Ops, SparseCore 0:
  10.1 112.3 all-gather.3
  170.4 104.1 reduce-scatter.1
where the time goes:
time: 282 us; the launch traced here: 281 us
  waiting for transfers between devices  202 us (72%)
  blocking collectives  46 us (16%)
  between operations  14.1 us (5%)
  matrix products  7.77 us (3%)
  starting transfers between devices  4.84 us (2%)
  other arithmetic  3.41 us (1%)
  local copies, waits for them, and re-layouts  3.12 us (1%)
    reduce_scatter x1, waiting for transfers between devices, body(): lax.psum_scatter(lax.dot_general(picked, weight_tile, (((1,), (1,)), ((),...  104 us
    all_gather x1, waiting for transfers between devices, body(): lax.all_gather(activations[0], 'col', axis=0, tiled=True)  85.1 us
    all_gather x2, blocking collectives, stacked_from(): pieces = lax.all_gather(pieces, axes[k])  29.3 us
    all_to_all x1, blocking collectives, from_everyone(): return lax.all_to_all(copies, axis, split_axis=0, concat_axis=0, tiled=True)  16.7 us
    all_to_all x1, waiting for transfers between devices, summed_on_arrival(): pieces = lax.all_to_all(split_up(array, dim, peers), axis, 0, 0, tiled=True)  12.2 us
  transfers between devices with their start and end apart: 3, of which 3 were waited for; matrix products, arithmetic and copies ran while one was open for 1% of the time, Pallas kernels for 0%

commit v1 on v0

--- a/solution.py
+++ b/solution.py
@@ -72,9 +72,15 @@
     weight_tile = weight_tile * keep_tile.astype(jnp.bfloat16)
     grad_group = gathered_by_axis(out_grads[0], ROW, (0, 1), 0)
     picked = grad_group
+    _fill_knots = lambda block_in, axis_key: jnp.concatenate(
+        lax.all_to_all(
+            jnp.stack([block_in for _ in range(lax.axis_size(axis_key))], 0), axis_key, 0, 0
+        ),
+        axis=0,
+    )
     tile_grad = (
         lax.dot_general(
-            lax.all_gather(activations[0], "col", axis=0, tiled=True),
+            _fill_knots(activations[0], "col"),
             picked,
             (((0,), (0,)), ((), ())),
             preferred_element_type=jnp.float32,

time: 282 us -> 299 us (1.060)
  the two profiles are of different devices: /device:TPU:2 before, /device:TPU:6 now
where the time goes in v1:
time: 299 us; the launch traced here: 298 us
  waiting for transfers between devices  146 us (49%)
  blocking collectives  107 us (36%)
  between operations  14.1 us (5%)
  starting transfers between devices  13.6 us (5%)
  matrix products  7.78 us (3%)
  local copies, waits for them, and re-layouts  6.57 us (2%)
  other arithmetic  3.42 us (1%)
    reduce_scatter x1, waiting for transfers between devices, body(): lax.psum_scatter(lax.dot_general(picked, weight_tile, (((1,), (1,)), ((),...  124 us
    all_gather x2, blocking collectives, stacked_from(): pieces = lax.all_gather(pieces, axes[k])  91.1 us
    all_to_all x1, blocking collectives, from_everyone(): return lax.all_to_all(copies, axis, split_axis=0, concat_axis=0, tiled=True)  15.6 us
    all_to_all x1, waiting for transfers between devices, body(): lax.all_to_all(jnp.stack([block_in for _ in range(lax.axis_size(axis_key)...  12 us
    all_to_all x1, waiting for transfers between devices, summed_on_arrival(): pieces = lax.all_to_all(split_up(array, dim, peers), axis, 0, 0, tiled=True)  10.5 us
    all_to_all x1, starting transfers between devices, body(): lax.all_to_all(jnp.stack([block_in for _ in range(lax.axis_size(axis_key)...  8.82 us
  transfers between devices with their start and end apart: 3, of which 3 were waited for; matrix products, arithmetic and copies ran while one was open for 1% of the time, Pallas kernels for 0%

profile of v1, /device:TPU:6, one launch (start us, length us, event | category | flops | bytes accessed | tf_op | source)
XLA Modules:
  0.0 298.3 jit_solution(3683302855720982733)
XLA Ops:
  7.2 3.4 %stack.3 = bf16[16,64,2048]{2,1,0:T(8,128)(2,1)} broadcast(bf16[64,2048]{1,0:T(8,128)(2,1)} %bitcast.31), dimensions={1,2} | broadcast | bytes 4456448 | tf_op jit(solution)/shard_map/stack | solution.py:77
  10.6 0.0 copy-start.2
  10.6 8.8 %all-to-all-start = ((bf16[16,64,2048]{2,1,0:T(8,128)(2,1)}), bf16[16,64,2048]{2,1,0:T(8,128)(2,1)}, u32[]{:S(2)}, u32[]{:S(2)}) async-start(bf16[16,64,2048]{2,1,0:T(8,128)(2,1)} %stack.3), calls=%async_computation | async-start | bytes 8388608 | tf_op jit(solution)/shard_map/all_to_all | solution.py:76
  19.4 0.0 copy-done.2
  19.4 0.0 copy-start.3
  19.5 88.9 %all_gather.9 = bf16[4,128,256]{2,1,0:T(8,128)(2,1)S(1)} all-gather(bf16[1,128,256]{2,1,0:T(8,128)(2,1)S(1)} %copy-done.2), channel_id=1, replica_groups=mesh['row_0'=4,'row_1'=2,'col'=16,'dp'=4] {'row_0'}, dimensions={0}, use_global_device_ids=true | all-gather | bytes 327680 | tf_op jit(solution)/shard_map/all_gather | solution.py:37
  108.4 2.2 all-gather
  110.6 0.0 copy-done.3
  110.6 0.0 copy-start
  110.6 0.1 copy.15
  110.7 12.0 %all-to-all-done = bf16[16,64,2048]{2,1,0:T(8,128)(2,1)} async-done(((bf16[16,64,2048]{2,1,0:T(8,128)(2,1)}), bf16[16,64,2048]{2,1,0:T(8,128)(2,1)}, u32[]{:S(2)}, u32[]{:S(2)}) %all-to-all-start) | async-done | bytes 4194336 | tf_op jit(solution)/shard_map/all_to_all | solution.py:76
  122.6 0.6 broadcast_in_dim.12
  123.3 4.5 %convolution_multiply_fusion = bf16[2048,256]{1,0:T(8,128)(2,1)} fusion(bf16[1024,2048]{1,0:T(8,128)(2,1)} %bitcast.4, bf16[1024,256]{1,0:T(8,128)(2,1)S(1)} %bitcast.26, f32[256,8,2,128]{3,2,1,0:T(2,128)S(1)} %bitcast.23), kind=kOutput, calls=%fused_computation.1 | convolution fusion | flops 1074790400 | bytes 7864320 | tf_op jit(solution)/shard_map/dot_general | solution.py:82
  127.8 0.0 copy-done
  127.8 4.8 %all-to-all-start.2 = ((bf16[4,512,256]{2,1,0:T(8,128)(2,1)}), bf16[4,512,256]{2,1,0:T(8,128)(2,1)S(1)}, u32[]{:S(2)}, u32[]{:S(2)}) async-start(bf16[4,512,256]{2,1,0:T(8,128)(2,1)} %bitcast.30), calls=%async_computation.3 | async-start | bytes 2097152 | tf_op jit(solution)/shard_map/all_to_all | solution.py:55
  132.6 0.0 reduce-scatter.2.cloned.1.call-start
  132.6 1.5 copy.22
  134.1 10.5 %all-to-all-done.2 = bf16[4,512,256]{2,1,0:T(8,128)(2,1)S(1)} async-done(((bf16[4,512,256]{2,1,0:T(8,128)(2,1)}), bf16[4,512,256]{2,1,0:T(8,128)(2,1)S(1)}, u32[]{:S(2)}, u32[]{:S(2)}) %all-to-all-start.2) | async-done | bytes 1048608 | tf_op jit(solution)/shard_map/all_to_all | solution.py:55
  144.5 0.1 convert_reduce_fusion
  144.7 3.1 %subtract_multiply_fusion = (f32[512,256]{1,0:T(8,128)}, f32[512,256]{1,0:T(8,128)}, f32[512,256]{1,0:T(8,128)}, bf16[512,256]{1,0:T(8,128)(2,1)S(1)}) fusion(f32[512,256]{1,0:T(8,128)} %param.9, f32[2048,256]{1,0:T(8,128)} %bitcast.28, s32[]{:T(128)S(6)} %select_n.3, f32[512,256]{1,0:T(8,128)S(1)} %convert_reduce_fusion, f32[512,256]{1,0:T(8,128)} %param.10, ...), kind=kLoop, calls=%fused_computation.7 | loop fusion | flops 1966080 | bytes 4456452 | tf_op jit(solution)/shard_map/mul | solution.py:105
  147.7 0.1 broadcast_in_dim.13
  147.8 15.6 %all_to_all.15 = bf16[4,512,256]{2,1,0:T(8,128)(2,1)S(1)} all-to-all(bf16[4,512,256]{2,1,0:T(8,128)(2,1)S(1)} %broadcast_in_dim.13), channel_id=1, replica_groups=mesh['row_0'=4,'row_1'=2,'col'=16,'dp'=4] {'dp'}, dimensions={0} | all-to-all | bytes 2097152 | tf_op jit(solution)/shard_map/all_to_all | solution.py:20
  163.4 0.0 copy-start.1
  163.4 0.2 bitcast_multiply_fusion
  163.6 0.8 copy-done.1
  164.4 3.2 %convolution_convert_fusion = bf16[1024,2048]{1,0:T(8,128)(2,1)} fusion(bf16[1024,256]{1,0:T(8,128)(2,1)S(1)} %bitcast.27, bf16[2048,256]{1,0:T(8,128)(2,1)S(1)} %bitcast_multiply_fusion), kind=kOutput, calls=%fused_computation | convolution fusion | flops 1075838976 | bytes 5767168 | tf_op jit(solution)/shard_map/dot_general | solution.py:93
  167.7 0.0 reduce-scatter.2.cloned.1.call-update
  167.7 123.8 %reduce-scatter.2.cloned.1.call-done = bf16[64,2048]{1,0:T(8,128)(2,1)} async-done(((bf16[1024,2048]{1,0:T(8,128)(2,1)}), bf16[64,2048]{1,0:T(8,128)(2,1)}) %reduce-scatter.2.cloned.1.call-update) | async-done | bytes 262160 | tf_op jit(solution)/shard_map/reduce_scatter | solution.py:92
  (2 shorter events, 0.0 us)
Async XLA Ops:
  10.6 8.8 %copy-start.2 = (bf16[1,128,256]{2,1,0:T(8,128)(2,1)S(1)}, bf16[1,128,256]{2,1,0:T(8,128)(2,1)}, u32[]{:S(2)}) copy-start(bf16[1,128,256]{2,1,0:T(8,128)(2,1)} %param.7) | copy-start | bytes 196612
  10.6 112.0 %all-to-all-start = ((bf16[16,64,2048]{2,1,0:T(8,128)(2,1)}), bf16[16,64,2048]{2,1,0:T(8,128)(2,1)}, u32[]{:S(2)}, u32[]{:S(2)}) async-start(bf16[16,64,2048]{2,1,0:T(8,128)(2,1)} %stack.3), calls=%async_computation | async-start | bytes 8388608 | tf_op jit(solution)/shard_map/all_to_all | solution.py:76
  19.4 91.1 %copy-start.3 = (s32[16,2]{0,1:T(2,128)S(1)}, s32[16,2]{0,1:T(2,128)}, u32[]{:S(2)}) copy-start(s32[16,2]{0,1:T(2,128)} %param.8) | copy-start | bytes 388
  110.6 17.2 %copy-start = (bf16[4,2,128,256]{3,2,1,0:T(8,128)(2,1)}, bf16[4,2,128,256]{3,2,1,0:T(8,128)(2,1)S(1)}, u32[]{:S(2)}) copy-start(bf16[4,2,128,256]{3,2,1,0:T(8,128)(2,1)S(1)} %copy.14) | copy-start | bytes 1572868
  127.8 16.7 %all-to-all-start.2 = ((bf16[4,512,256]{2,1,0:T(8,128)(2,1)}), bf16[4,512,256]{2,1,0:T(8,128)(2,1)S(1)}, u32[]{:S(2)}, u32[]{:S(2)}) async-start(bf16[4,512,256]{2,1,0:T(8,128)(2,1)} %bitcast.30), calls=%async_computation.3 | async-start | bytes 2097152 | tf_op jit(solution)/shard_map/all_to_all | solution.py:55
  132.6 158.9 %reduce-scatter.2.cloned.1.call-start = ((), (), s32[]{:S(2)}) async-start(), calls=%async_computation.4 | async-start | bytes 4456448 | tf_op jit(solution)/shard_map/reduce_scatter | solution.py:92
  163.4 1.0 copy-start.1
Sparse Core Ops, SparseCore 0:
  167.8 123.6 reduce-scatter.1
